TPU v7x, 32 devices: a whole 2x2x4 slice. The times are simulated.
32 devices in a mesh: gx: 4 (over z), gy: 4 (over x, core), gz: 2 (over y).
Axes of the slice: x: 2, y: 2, z: 4, core: 2. Of those that a mesh axis runs over, the one named last changes fastest.
Arguments:
- weights: float32 [3, 16, 128, 512], P(None, 'gx', 'gz', 'gy'), may hold values from 0.2 to 2
- abscissas: float32 [3, 16, 128, 512], P(None, 'gx', 'gz', 'gy'), may hold values from -4 to 4, as said below
Outputs:
- moments_end: float32 [6, 16, 128, 512], P(None, 'gx', 'gz', 'gy')
Inputs may be any that keep to these rules, and one draw needn't show every extreme that they name: In every cell the three abscissas increase with the node index, consecutive ones at least 0.25 apart.
All inputs are finite; a program needn't handle non-finite values. Where the computation divides by a largest or mean magnitude, that divisor is 1e-20 or more.
Results may differ from a plain program's by a relative error of at most 0.0003.
Values sent between devices are 32-bit elements; how exact they have to be, the bound alone decides.
A program may use at most 128 MiB of HBM per device.

v0:
```python
import math

import jax
import jax.numpy as jnp
from jax import lax
from jax.sharding import PartitionSpec as P

COURANT = 0.4
SPEED_TOTAL = 1.72
AXIS_SPEEDS = ((1, 0.6), (2, 0.64), (3, 0.48))


def with_halo(value, sides, width):
    for axis, dim in sides:
        count, length = (lax.axis_size(axis), value.shape[dim])
        up = [(i, (i + 1) % count) for i in range(count)]
        down = [(j, i) for i, j in up]
        last = lax.slice_in_dim(value, length - width, length, axis=dim)
        initial = lax.slice_in_dim(value, 0, width, axis=dim)
        before = lax.ppermute(last, axis, up)
        after = lax.ppermute(initial, axis, down)
        value = jnp.concatenate([before, value, after], axis=dim)
    return value


def minmod(first, second):
    return jnp.where(
        first * second > 0.0, jnp.sign(first) * jnp.minimum(jnp.abs(first), jnp.abs(second)), 0.0
    )


def cut_along(array, lower, upper, array_axis):
    return lax.slice_in_dim(array, lower, upper, axis=array_axis)


def moments_of(node_weights, node_speeds):
    result = []
    power = node_weights
    for order in range(6):
        result.append(jnp.sum(power, axis=0))
        power = power * node_speeds
    return jnp.stack(result)


def face_divergence(node_weights, node_speeds):
    total = None
    for array_axis, component in AXIS_SPEEDS:
        window = [slice(None), slice(2, -2), slice(2, -2), slice(2, -2)]
        window[array_axis] = slice(None)
        line_w = node_weights[tuple(window)]
        line_u = node_speeds[tuple(window)]
        length = line_w.shape[array_axis]
        jumps = cut_along(line_w, 1, length, array_axis) - cut_along(
            line_w, 0, length - 1, array_axis
        )
        slopes = minmod(
            cut_along(jumps, 0, length - 2, array_axis), cut_along(jumps, 1, length - 1, array_axis)
        )
        left_w = cut_along(line_w, 1, length - 2, array_axis) + 0.5 * cut_along(
            slopes, 0, length - 3, array_axis
        )
        right_w = cut_along(line_w, 2, length - 1, array_axis) - 0.5 * cut_along(
            slopes, 1, length - 2, array_axis
        )
        left_u = cut_along(line_u, 1, length - 2, array_axis)
        right_u = cut_along(line_u, 2, length - 1, array_axis)
        left_term = component * left_w * jnp.maximum(left_u, 0.0)
        right_term = component * right_w * jnp.minimum(right_u, 0.0)
        fluxes = []
        for order in range(6):
            fluxes.append(jnp.sum(left_term + right_term, axis=0))
            left_term = left_term * left_u
            right_term = right_term * right_u
        flux = jnp.stack(fluxes)
        faces = length - 3
        diverge = cut_along(flux, 1, faces, array_axis) - cut_along(flux, 0, faces - 1, array_axis)
        total = diverge if total is None else total + diverge
    return total


def invert(moments):
    mom = [moments[index] for index in range(6)]
    mean_one = mom[1] / mom[0]
    first_row = [None] + [mom[level + 1] - mean_one * mom[level] for level in range(1, 5)]
    mean_two = first_row[2] / first_row[1] - mean_one
    spread_one = first_row[1] / mom[0]
    second_two = first_row[3] - mean_two * first_row[2] - spread_one * mom[2]
    second_three = first_row[4] - mean_two * first_row[3] - spread_one * mom[3]
    mean_three = second_three / second_two - first_row[2] / first_row[1]
    spread_two = second_two / first_row[1]
    centre = (mean_one + mean_two + mean_three) / 3.0
    dev_one = mean_one - centre
    dev_two = mean_two - centre
    dev_three = mean_three - centre
    radius = jnp.sqrt(
        (
            dev_one * dev_one
            + dev_two * dev_two
            + dev_three * dev_three
            + 2.0 * spread_one
            + 2.0 * spread_two
        )
        / 6.0
    )
    determinant = dev_one * dev_two * dev_three - dev_one * spread_two - dev_three * spread_one
    ratio = determinant / (2.0 * radius * radius * radius)
    angle = jnp.arccos(ratio) / 3.0
    highest = centre + 2.0 * radius * jnp.cos(angle)
    lowest = centre + 2.0 * radius * jnp.cos(angle + 2.0 * math.pi / 3.0)
    middle = 3.0 * centre - highest - lowest
    root_one = jnp.sqrt(spread_one)
    root_two = jnp.sqrt(spread_two)
    speeds = []
    masses = []
    for value in (lowest, middle, highest):
        first_comp = (value - mean_one) / root_one
        second_comp = ((value - mean_two) * first_comp - root_one) / root_two
        masses.append(mom[0] / (1.0 + first_comp * first_comp + second_comp * second_comp))
        speeds.append(value)
    return (jnp.stack(masses), jnp.stack(speeds))


def inner_cells(array):
    return array[:, 2:-2, 2:-2, 2:-2]


def local(weights, abscissas):
    moments_start = moments_of(weights, abscissas)
    fastest = lax.pmax(jnp.max(jnp.abs(abscissas)), ("gx", "gy", "gz"))
    step_one = COURANT / (SPEED_TOTAL * fastest)
    entry_w, entry_u = (
        with_halo(weights, (("gx", 1), ("gy", 3), ("gz", 2)), 2),
        with_halo(abscissas, (("gx", 1), ("gy", 3), ("gz", 2)), 2),
    )
    moments_mid = moments_start - step_one * face_divergence(entry_w, entry_u)
    wide_mid = with_halo(moments_mid, (("gx", 1), ("gy", 3), ("gz", 2)), 2)
    padded_w, padded_u = invert(wide_mid)
    inner_speeds = inner_cells(padded_u)
    fastest_mid = lax.pmax(jnp.max(jnp.abs(inner_speeds)), ("gx", "gy", "gz"))
    step_two = COURANT / (SPEED_TOTAL * fastest_mid)
    change = face_divergence(padded_w, padded_u)
    return 0.5 * moments_start + 0.5 * (moments_mid - step_two * change)


def solution(mesh):
    in_specs = (P(None, "gx", "gz", "gy"), P(None, "gx", "gz", "gy"))
    out_specs = P(None, "gx", "gz", "gy")
    return jax.shard_map(local, mesh=mesh, in_specs=in_specs, out_specs=out_specs, check_vma=False)
```

profile of v0, /device:TPU:0, one launch (start us, length us, event | category | flops | bytes accessed | tf_op | source)
XLA Modules:
  0.0 210.1 jit_solution(10886402759289722665)
XLA Ops:
  0.0 1.1 fusion.70
  1.1 3.1 %collective-permute-start.2 = (f32[3,2,64,128]{3,2,1,0:T(8,128)S(1)}, f32[3,2,64,128]{3,2,1,0:T(8,128)S(1)}, u32[]{:S(2)}, u32[]{:S(2)}) collective-permute-start(f32[3,2,64,128]{3,2,1,0:T(8,128)S(1)} %get-tuple-element.94), channel_id=1, source_target_pairs={{0,8},{8,16},{16,24},{24,0},{1,9},{9,17},{17,25},{25,1},{2,10},{10... | collective-permute-start | bytes 589832 | tf_op jit(solution)/shard_map/ppermute | solution.py:20
  5.3 1.6 collective-permute-start
  6.9 2.2 %collective-permute-start.1 = (f32[3,2,64,128]{3,2,1,0:T(8,128)S(1)}, f32[3,2,64,128]{3,2,1,0:T(8,128)S(1)}, u32[]{:S(2)}, u32[]{:S(2)}) collective-permute-start(f32[3,2,64,128]{3,2,1,0:T(8,128)S(1)} %get-tuple-element.97), channel_id=1, source_target_pairs={{8,0},{16,8},{24,16},{0,24},{9,1},{17,9},{25,17},{1,25},{10,2},{18... | collective-permute-start | bytes 589832 | tf_op jit(solution)/shard_map/ppermute | solution.py:21
  9.5 2.7 %collective-permute-done.2 = f32[3,2,64,128]{3,2,1,0:T(8,128)S(1)} collective-permute-done((f32[3,2,64,128]{3,2,1,0:T(8,128)S(1)}, f32[3,2,64,128]{3,2,1,0:T(8,128)S(1)}, u32[]{:S(2)}, u32[]{:S(2)}) %collective-permute-start.2) | collective-permute-done | bytes 196640 | tf_op jit(solution)/shard_map/ppermute | solution.py:20
  12.1 4.1 %collective-permute-done = f32[3,2,64,128]{3,2,1,0:T(8,128)S(1)} collective-permute-done((f32[3,2,64,128]{3,2,1,0:T(8,128)S(1)}, f32[3,2,64,128]{3,2,1,0:T(8,128)S(1)}, u32[]{:S(2)}, u32[]{:S(2)}) %collective-permute-start) | collective-permute-done | bytes 196640 | tf_op jit(solution)/shard_map/ppermute | solution.py:20
  16.3 1.1 multiply_reduce_fusion
  17.4 2.3 %collective-permute-done.1 = f32[3,2,64,128]{3,2,1,0:T(8,128)S(1)} collective-permute-done((f32[3,2,64,128]{3,2,1,0:T(8,128)S(1)}, f32[3,2,64,128]{3,2,1,0:T(8,128)S(1)}, u32[]{:S(2)}, u32[]{:S(2)}) %collective-permute-start.1) | collective-permute-done | bytes 196640 | tf_op jit(solution)/shard_map/ppermute | solution.py:21
  19.8 1.2 fusion.69
  21.2 2.6 %collective-permute-done.3 = f32[3,2,64,128]{3,2,1,0:T(8,128)S(1)} collective-permute-done((f32[3,2,64,128]{3,2,1,0:T(8,128)S(1)}, f32[3,2,64,128]{3,2,1,0:T(8,128)S(1)}, u32[]{:S(2)}, u32[]{:S(2)}) %collective-permute-start.3) | collective-permute-done | bytes 196640 | tf_op jit(solution)/shard_map/ppermute | solution.py:21
  24.7 1.1 add_reduce_fusion.18
  26.5 1.4 fusion.68
  27.9 1.4 copy.188
  29.3 1.4 copy.189
  30.8 1.1 collective-permute-start.9
  31.9 2.0 copy.179
  34.8 1.7 collective-permute-start.5
  40.3 1.6 bitcast_dynamic-update-slice_fusion.22
  41.9 1.6 bitcast_dynamic-update-slice_fusion.21
  45.5 40.6 %pmax.14 = f32[]{:T(128)} all-reduce(f32[]{:T(128)} %get-tuple-element.45), channel_id=1, replica_groups=mesh['gx'=4,'gy'=4,'gz'=2] {'gx','gy','gz'}, use_global_device_ids=true, to_apply=%region_7.0 | all-reduce | flops 1 | bytes 8 | tf_op jit(solution)/shard_map/pmax | solution.py:129
  88.2 1.8 pad_maximum_fusion.3
  90.3 1.9 copy.190
  92.2 1.2 copy.191
  93.4 1.4 pad_maximum_fusion.36
  94.8 2.6 %collective-permute-start.11 = (f32[3,8,2,132]{3,1,2,0:T(8,128)S(1)}, f32[3,8,2,132]{3,1,2,0:T(8,128)S(1)}, u32[]{:S(2)}, u32[]{:S(2)}) collective-permute-start(f32[3,8,2,132]{3,1,2,0:T(8,128)S(1)} %copy.195), channel_id=1, source_target_pairs={{1,0},{0,1},{3,2},{2,3},{5,4},{4,5},{7,6},{6,7},{9,8},{8,9},{11,10... | collective-permute-start | bytes 76040 | tf_op jit(solution)/shard_map/ppermute | solution.py:21
  97.5 2.0 collective-permute-start.7
  106.8 1.7 collective-permute-start.12
  108.4 2.2 %collective-permute-start.13 = (f32[6,2,64,128]{3,2,1,0:T(8,128)S(1)}, f32[6,2,64,128]{3,2,1,0:T(8,128)S(1)}, u32[]{:S(2)}, u32[]{:S(2)}) collective-permute-start(f32[6,2,64,128]{3,2,1,0:T(8,128)S(1)} %get-tuple-element.88), channel_id=1, source_target_pairs={{8,0},{16,8},{24,16},{0,24},{9,1},{17,9},{25,17},{1,25},{10,2},{18... | collective-permute-start | bytes 1179656 | tf_op jit(solution)/shard_map/ppermute | solution.py:21
  110.7 10.0 %collective-permute-done.12 = f32[6,2,64,128]{3,2,1,0:T(8,128)S(1)} collective-permute-done((f32[6,2,64,128]{3,2,1,0:T(8,128)S(1)}, f32[6,2,64,128]{3,2,1,0:T(8,128)S(1)}, u32[]{:S(2)}, u32[]{:S(2)}) %collective-permute-start.12) | collective-permute-done | bytes 393248 | tf_op jit(solution)/shard_map/ppermute | solution.py:20
  120.6 4.0 %collective-permute-done.13 = f32[6,2,64,128]{3,2,1,0:T(8,128)S(1)} collective-permute-done((f32[6,2,64,128]{3,2,1,0:T(8,128)S(1)}, f32[6,2,64,128]{3,2,1,0:T(8,128)S(1)}, u32[]{:S(2)}, u32[]{:S(2)}) %collective-permute-start.13) | collective-permute-done | bytes 393248 | tf_op jit(solution)/shard_map/ppermute | solution.py:21
  124.8 1.7 fusion.66
  126.5 1.9 copy.225
  129.0 1.8 collective-permute-start.15
  130.8 1.2 collective-permute-done.14
  132.5 1.7 copy.228
  134.2 1.5 pad_maximum_fusion.33
  135.8 1.4 collective-permute-start.17
  137.9 3.1 %collective-permute-done.17 = f32[6,8,2,132]{3,1,2,0:T(8,128)S(1)} collective-permute-done((f32[6,8,2,132]{3,1,2,0:T(8,128)S(1)}, f32[6,8,2,132]{3,1,2,0:T(8,128)S(1)}, u32[]{:S(2)}, u32[]{:S(2)}) %collective-permute-start.17) | collective-permute-done | bytes 50720 | tf_op jit(solution)/shard_map/ppermute | solution.py:21
  141.1 2.1 collective-permute-done.16
  143.2 2.2 %pad_maximum_fusion = f32[6,8,68,132]{3,2,1,0:T(8,128)S(1)} fusion(f32[6,8,2,132]{3,2,1,0:T(2,128)S(1)} %copy.232, f32[6,8,64,2]{3,2,1,0:T(8,128)S(1)} %copy-done.2, f32[6,2,64,128]{3,2,1,0:T(8,128)S(1)} %collective-permute-done.13, f32[6,4,64,128]{3,2,1,0:T(8,128)S(1)} %fusion.14, f32[6,2,64,128]{3,2,1,0:T(8,128)S(1)} %collective-permute-done.12, ...), kind=kLoop, calls=%fused_computation | loop fusion | flops 2585088 | bytes 3446784 | tf_op jit(solution)/shard_map/concatenate | solution.py:22
  145.6 4.8 %add_divide_fusion.2 = (f32[1,8,68,132]{3,2,1,0:T(8,128)S(1)}, f32[1,8,68,132]{3,2,1,0:T(8,128)S(1)}, f32[1,8,68,132]{3,2,1,0:T(8,128)S(1)}, f32[1,8,68,132]{3,2...) fusion(f32[1,8,68,132]{3,2,1,0:T(8,128)S(1)} %get-tuple-element.57, ...), kind=kLoop, calls=%fused_computation.80 | loop fusion | flops 4595712 | bytes 3734016 | tf_op jit(solution)/shard_map/div | solution.py:118
  150.3 4.3 %add_divide_fusion.1 = (f32[1,8,68,132]{3,2,1,0:T(8,128)S(1)}, f32[1,8,68,132]{3,2,1,0:T(8,128)S(1)}, f32[1,8,68,132]{3,2,1,0:T(8,128)S(1)}) fusion(f32[1,8,68,132]{3,2,1,0:T(8,128)S(1)} %get-tuple-element.51, f32[1,8,68,132]{3,2,1,0:T(8,128)S(1)} %get-tuple-element.57, f32[1,8,68,132]{3,2,1,0:T(8,128)S(1)} %get-tuple-element.50, ...), kind=kLoop, calls=%fused_computation.79 | loop fusion | flops 3231360 | bytes 2872320 | tf_op jit(solution)/shard_map/div | solution.py:118
  156.2 1.1 multiply_select_fusion.2
  157.3 1.3 multiply_select_fusion
  160.5 40.2 %pmax.15 = f32[]{:T(128)} all-reduce(f32[]{:T(128)} %fusion.54), channel_id=1, replica_groups=mesh['gx'=4,'gy'=4,'gz'=2] {'gx','gy','gz'}, use_global_device_ids=true, to_apply=%region_27.28 | all-reduce | flops 1 | bytes 8 | tf_op jit(solution)/shard_map/pmax | solution.py:139
  201.4 1.8 fusion.31
  204.4 1.1 fusion.7
  208.8 1.3 fusion.4
  (138 shorter events, 28.5 us)
Async XLA Ops:
  0.0 16.3 %copy-start.6 = (f32[3,4,64,128]{3,2,1,0:T(8,128)S(1)}, f32[3,4,64,128]{3,2,1,0:T(8,128)}, u32[]{:S(2)}) copy-start(f32[3,4,64,128]{3,2,1,0:T(8,128)} %param.3) | copy-start | bytes 1179652
  0.0 16.3 %copy-start.12 = (f32[3,4,64,128]{3,2,1,0:T(8,128)S(1)}, f32[3,4,64,128]{3,2,1,0:T(8,128)}, u32[]{:S(2)}) copy-start(f32[3,4,64,128]{3,2,1,0:T(8,128)} %param.2) | copy-start | bytes 1179652
  1.1 11.0 %collective-permute-start.2 = (f32[3,2,64,128]{3,2,1,0:T(8,128)S(1)}, f32[3,2,64,128]{3,2,1,0:T(8,128)S(1)}, u32[]{:S(2)}, u32[]{:S(2)}) collective-permute-start(f32[3,2,64,128]{3,2,1,0:T(8,128)S(1)} %get-tuple-element.94), channel_id=1, source_target_pairs={{0,8},{8,16},{16,24},{24,0},{1,9},{9,17},{17,25},{25,1},{2,10},{10... | collective-permute-start | bytes 589832 | tf_op jit(solution)/shard_map/ppermute | solution.py:20
  5.3 11.0 %collective-permute-start = (f32[3,2,64,128]{3,2,1,0:T(8,128)S(1)}, f32[3,2,64,128]{3,2,1,0:T(8,128)S(1)}, u32[]{:S(2)}, u32[]{:S(2)}) collective-permute-start(f32[3,2,64,128]{3,2,1,0:T(8,128)S(1)} %get-tuple-element.98), channel_id=1, source_target_pairs={{0,8},{8,16},{16,24},{24,0},{1,9},{9,17},{17,25},{25,1},{2,10},{10... | collective-permute-start | bytes 589832 | tf_op jit(solution)/shard_map/ppermute | solution.py:20
  6.9 12.8 %collective-permute-start.1 = (f32[3,2,64,128]{3,2,1,0:T(8,128)S(1)}, f32[3,2,64,128]{3,2,1,0:T(8,128)S(1)}, u32[]{:S(2)}, u32[]{:S(2)}) collective-permute-start(f32[3,2,64,128]{3,2,1,0:T(8,128)S(1)} %get-tuple-element.97), channel_id=1, source_target_pairs={{8,0},{16,8},{24,16},{0,24},{9,1},{17,9},{25,17},{1,25},{10,2},{18... | collective-permute-start | bytes 589832 | tf_op jit(solution)/shard_map/ppermute | solution.py:21
  9.2 14.6 %collective-permute-start.3 = (f32[3,2,64,128]{3,2,1,0:T(8,128)S(1)}, f32[3,2,64,128]{3,2,1,0:T(8,128)S(1)}, u32[]{:S(2)}, u32[]{:S(2)}) collective-permute-start(f32[3,2,64,128]{3,2,1,0:T(8,128)S(1)} %get-tuple-element.93), channel_id=1, source_target_pairs={{8,0},{16,8},{24,16},{0,24},{9,1},{17,9},{25,17},{1,25},{10,2},{18... | collective-permute-start | bytes 589832 | tf_op jit(solution)/shard_map/ppermute | solution.py:21
  30.8 61.4 %collective-permute-start.9 = (f32[3,8,64,2]{2,1,3,0:T(8,128)S(1)}, f32[3,8,64,2]{2,1,3,0:T(8,128)S(1)}, u32[]{:S(2)}, u32[]{:S(2)}) collective-permute-start(f32[3,8,64,2]{2,1,3,0:T(8,128)S(1)} %copy.189), channel_id=1, source_target_pairs={{2,0},{4,2},{6,4},{0,6},{3,1},{5,3},{7,5},{1,7},{10,8},{12,10},{14... | collective-permute-start | bytes 36872 | tf_op jit(solution)/shard_map/ppermute | solution.py:21
  31.9 58.3 %collective-permute-start.8 = (f32[3,8,64,2]{2,1,3,0:T(8,128)S(1)}, f32[3,8,64,2]{2,1,3,0:T(8,128)}, u32[]{:S(2)}, u32[]{:S(2)}) collective-permute-start(f32[3,8,64,2]{2,1,3,0:T(8,128)S(1)} %copy.188), channel_id=1, source_target_pairs={{0,2},{2,4},{4,6},{6,0},{1,3},{3,5},{5,7},{7,1},{8,10},{10,12},{12... | collective-permute-start | bytes 36872 | tf_op jit(solution)/shard_map/ppermute | solution.py:20
  34.8 8.6 %copy-start.14 = (f32[5,64,128]{2,1,0:T(8,128)S(1)}, f32[5,64,128]{2,1,0:T(8,128)}, u32[]{:S(2)}) copy-start(f32[5,64,128]{2,1,0:T(8,128)} %get-tuple-element.28) | copy-start | bytes 491524
  34.8 10.6 %copy-start.15 = (f32[4,64,128]{2,1,0:T(8,128)S(1)}, f32[4,64,128]{2,1,0:T(8,128)}, u32[]{:S(2)}) copy-start(f32[4,64,128]{2,1,0:T(8,128)} %get-tuple-element.40) | copy-start | bytes 393220
  34.8 52.3 %collective-permute-start.5 = (f32[3,8,64,2]{2,1,3,0:T(8,128)}, f32[3,8,64,2]{2,1,3,0:T(8,128)}, u32[]{:S(2)}, u32[]{:S(2)}) collective-permute-start(f32[3,8,64,2]{2,1,3,0:T(8,128)} %copy.180), channel_id=1, source_target_pairs={{2,0},{4,2},{6,4},{0,6},{3,1},{5,3},{7,5},{1,7},{10,8},{12,10},{14... | collective-permute-start | bytes 36872 | tf_op jit(solution)/shard_map/ppermute | solution.py:21
  36.6 50.2 %collective-permute-start.4 = (f32[3,8,64,2]{2,1,3,0:T(8,128)}, f32[3,8,64,2]{2,1,3,0:T(8,128)S(1)}, u32[]{:S(2)}, u32[]{:S(2)}) collective-permute-start(f32[3,8,64,2]{2,1,3,0:T(8,128)} %copy.179), channel_id=1, source_target_pairs={{0,2},{2,4},{4,6},{6,0},{1,3},{3,5},{5,7},{7,1},{8,10},{10,12},{12... | collective-permute-start | bytes 36872 | tf_op jit(solution)/shard_map/ppermute | solution.py:20
  45.5 41.3 %copy-start.9 = (f32[6,4,64,128]{3,2,1,0:T(8,128)}, f32[6,4,64,128]{3,2,1,0:T(8,128)S(1)}, u32[]{:S(2)}) copy-start(f32[6,4,64,128]{3,2,1,0:T(8,128)S(1)} %bitcast_dynamic-update-slice_fusion.36) | copy-start | bytes 2359300
  93.4 6.2 %copy-start.7 = (f32[3,8,64,132]{3,2,1,0:T(8,128)S(1)}, f32[3,8,64,132]{3,2,1,0:T(8,128)}, u32[]{:S(2)}) copy-start(f32[3,8,64,132]{3,2,1,0:T(8,128)} %pad_maximum_fusion.3) | copy-start | bytes 2433028
  94.8 9.4 %collective-permute-start.11 = (f32[3,8,2,132]{3,1,2,0:T(8,128)S(1)}, f32[3,8,2,132]{3,1,2,0:T(8,128)S(1)}, u32[]{:S(2)}, u32[]{:S(2)}) collective-permute-start(f32[3,8,2,132]{3,1,2,0:T(8,128)S(1)} %copy.195), channel_id=1, source_target_pairs={{1,0},{0,1},{3,2},{2,3},{5,4},{4,5},{7,6},{6,7},{9,8},{8,9},{11,10... | collective-permute-start | bytes 76040 | tf_op jit(solution)/shard_map/ppermute | solution.py:21
  97.4 6.9 %collective-permute-start.10 = (f32[3,8,2,132]{3,1,2,0:T(8,128)S(1)}, f32[3,8,2,132]{3,1,2,0:T(8,128)S(1)}, u32[]{:S(2)}, u32[]{:S(2)}) collective-permute-start(f32[3,8,2,132]{3,1,2,0:T(8,128)S(1)} %copy.192), channel_id=1, source_target_pairs={{0,1},{1,0},{2,3},{3,2},{4,5},{5,4},{6,7},{7,6},{8,9},{9,8},{10,11... | collective-permute-start | bytes 76040 | tf_op jit(solution)/shard_map/ppermute | solution.py:20
  97.5 5.5 %collective-permute-start.7 = (f32[3,8,2,132]{3,1,2,0:T(8,128)S(1)}, f32[3,8,2,132]{3,1,2,0:T(8,128)S(1)}, u32[]{:S(2)}, u32[]{:S(2)}) collective-permute-start(f32[3,8,2,132]{3,1,2,0:T(8,128)S(1)} %copy.185), channel_id=1, source_target_pairs={{1,0},{0,1},{3,2},{2,3},{5,4},{4,5},{7,6},{6,7},{9,8},{8,9},{11,10... | collective-permute-start | bytes 76040 | tf_op jit(solution)/shard_map/ppermute | solution.py:21
  99.5 4.1 %collective-permute-start.6 = (f32[3,8,2,132]{3,1,2,0:T(8,128)S(1)}, f32[3,8,2,132]{3,1,2,0:T(8,128)S(1)}, u32[]{:S(2)}, u32[]{:S(2)}) collective-permute-start(f32[3,8,2,132]{3,1,2,0:T(8,128)S(1)} %copy.183), channel_id=1, source_target_pairs={{0,1},{1,0},{2,3},{3,2},{4,5},{5,4},{6,7},{7,6},{8,9},{9,8},{10,11... | collective-permute-start | bytes 76040 | tf_op jit(solution)/shard_map/ppermute | solution.py:20
  99.9 1.1 copy-start.3
  99.9 1.4 copy-start.4
  104.9 1.1 copy-start.10
  104.9 1.4 copy-start.13
  106.7 36.5 %copy-start = (f32[6,4,64,128]{3,2,1,0:T(8,128)}, f32[6,4,64,128]{3,2,1,0:T(8,128)S(1)}, u32[]{:S(2)}) copy-start(f32[6,4,64,128]{3,2,1,0:T(8,128)S(1)} %fusion.14) | copy-start | bytes 2359300
  106.8 13.8 %collective-permute-start.12 = (f32[6,2,64,128]{3,2,1,0:T(8,128)S(1)}, f32[6,2,64,128]{3,2,1,0:T(8,128)S(1)}, u32[]{:S(2)}, u32[]{:S(2)}) collective-permute-start(f32[6,2,64,128]{3,2,1,0:T(8,128)S(1)} %get-tuple-element.87), channel_id=1, source_target_pairs={{0,8},{8,16},{16,24},{24,0},{1,9},{9,17},{17,25},{25,1},{2,10},{10... | collective-permute-start | bytes 1179656 | tf_op jit(solution)/shard_map/ppermute | solution.py:20
  108.4 16.2 %collective-permute-start.13 = (f32[6,2,64,128]{3,2,1,0:T(8,128)S(1)}, f32[6,2,64,128]{3,2,1,0:T(8,128)S(1)}, u32[]{:S(2)}, u32[]{:S(2)}) collective-permute-start(f32[6,2,64,128]{3,2,1,0:T(8,128)S(1)} %get-tuple-element.88), channel_id=1, source_target_pairs={{8,0},{16,8},{24,16},{0,24},{9,1},{17,9},{25,17},{1,25},{10,2},{18... | collective-permute-start | bytes 1179656 | tf_op jit(solution)/shard_map/ppermute | solution.py:21
  128.4 3.5 %collective-permute-start.14 = (f32[6,8,64,2]{2,1,3,0:T(8,128)S(1)}, f32[6,8,64,2]{2,1,3,0:T(8,128)S(1)}, u32[]{:S(2)}, u32[]{:S(2)}) collective-permute-start(f32[6,8,64,2]{2,1,3,0:T(8,128)S(1)} %copy.225), channel_id=1, source_target_pairs={{0,2},{2,4},{4,6},{6,0},{1,3},{3,5},{5,7},{7,1},{8,10},{10,12},{12... | collective-permute-start | bytes 73736 | tf_op jit(solution)/shard_map/ppermute | solution.py:20
  129.0 3.5 %collective-permute-start.15 = (f32[6,8,64,2]{2,1,3,0:T(8,128)S(1)}, f32[6,8,64,2]{2,1,3,0:T(8,128)S(1)}, u32[]{:S(2)}, u32[]{:S(2)}) collective-permute-start(f32[6,8,64,2]{2,1,3,0:T(8,128)S(1)} %copy.226), channel_id=1, source_target_pairs={{2,0},{4,2},{6,4},{0,6},{3,1},{5,3},{7,5},{1,7},{10,8},{12,10},{14... | collective-permute-start | bytes 73736 | tf_op jit(solution)/shard_map/ppermute | solution.py:21
  134.2 8.9 %copy-start.2 = (f32[6,8,64,2]{3,2,1,0:T(8,128)S(1)}, f32[6,8,64,2]{3,2,1,0:T(8,128)}, u32[]{:S(2)}) copy-start(f32[6,8,64,2]{3,2,1,0:T(8,128)} %copy.228) | copy-start | bytes 73732
  135.8 5.2 %collective-permute-start.17 = (f32[6,8,2,132]{3,1,2,0:T(8,128)S(1)}, f32[6,8,2,132]{3,1,2,0:T(8,128)S(1)}, u32[]{:S(2)}, u32[]{:S(2)}) collective-permute-start(f32[6,8,2,132]{3,1,2,0:T(8,128)S(1)} %copy.230), channel_id=1, source_target_pairs={{1,0},{0,1},{3,2},{2,3},{5,4},{4,5},{7,6},{6,7},{9,8},{8,9},{11,10... | collective-permute-start | bytes 152072 | tf_op jit(solution)/shard_map/ppermute | solution.py:21
  137.2 5.9 %collective-permute-start.16 = (f32[6,8,2,132]{3,1,2,0:T(8,128)S(1)}, f32[6,8,2,132]{3,1,2,0:T(8,128)S(1)}, u32[]{:S(2)}, u32[]{:S(2)}) collective-permute-start(f32[6,8,2,132]{3,1,2,0:T(8,128)S(1)} %copy.229), channel_id=1, source_target_pairs={{0,1},{1,0},{2,3},{3,2},{4,5},{5,4},{6,7},{7,6},{8,9},{9,8},{10,11... | collective-permute-start | bytes 152072 | tf_op jit(solution)/shard_map/ppermute | solution.py:20
  201.4 1.9 copy-start.8
  203.3 1.1 copy-start.5
  207.4 1.1 copy-start.1
  207.4 1.4 copy-start.11
where the time goes:
time: 211 us; the launch traced here: 210 us
  blocking collectives  80.8 us (38%)
  other arithmetic  36.4 us (17%)
  local copies, waits for them, and re-layouts  35.6 us (17%)
  waiting for transfers between devices  32.5 us (15%)
  starting transfers between devices  22.7 us (11%)
  between operations  2.12 us (1%)
    pmax x1, blocking collectives, local(): fastest = lax.pmax(jnp.max(jnp.abs(abscissas)), ('gx', 'gy', 'gz'))  40.6 us
    pmax x1, blocking collectives, local(): fastest_mid = lax.pmax(jnp.max(jnp.abs(inner_speeds)), ('gx', 'gy', 'gz'))  40.2 us
    ppermute x9, waiting for transfers between devices, with_halo(): before = lax.ppermute(last, axis, up)  20.6 us
    ppermute x9, starting transfers between devices, with_halo(): after = lax.ppermute(initial, axis, down)  15.4 us
    unnamed x69, local copies, waits for them, and re-layouts  13 us
    ppermute x9, waiting for transfers between devices, with_halo(): after = lax.ppermute(initial, axis, down)  12 us
    slice x10, local copies, waits for them, and re-layouts, with_halo(): last = lax.slice_in_dim(value, length - width, length, axis=dim)  9.78 us
    div x3, other arithmetic, invert(): mom[0] / (1.0 + first_comp * first_comp + second_comp * second_comp)  9.51 us
  transfers between devices with their start and end apart: 18, of which 10 were waited for; matrix products, arithmetic and copies ran while one was open for 12% of the time, Pallas kernels for 0%

commit v1 on v0

v1 whole, which is shorter than its diff:
```python
import functools

import jax
import jax.numpy as jnp
from jax import lax
from jax.experimental import pallas as pl
from jax.experimental.pallas import tpu as pltpu
from jax.sharding import PartitionSpec as P

MESH = pl.DeviceIdType.MESH
COURANT = 0.4
SPEED_TOTAL = 1.72
CX, CZ, CY = 0.6, 0.64, 0.48
COS_COEFFS = (
    0.500000001, 0.57735016, -0.111107418, 0.0534091939, -0.032581471,
    0.0214679648, -0.0133677689, 0.00671727328, -0.00224476683, 0.000356832615,
)
ROWS = 8


def minmod(a, b):
    return jnp.maximum(jnp.minimum(a, b), 0.0) + jnp.minimum(jnp.maximum(a, b), 0.0)


def third_cos(t):
    acc = jnp.full_like(t, COS_COEFFS[-1])
    for c in COS_COEFFS[-2::-1]:
        acc = acc * t + c
    return acc


def total(parts):
    return parts[0] + parts[1] + parts[2]


def shift(value, amount, axis):
    return pltpu.roll(value, amount % value.shape[axis], axis)


def edge_terms(own, left, right, axis, c):
    shape = own(0).shape
    q = lax.broadcasted_iota(jnp.int32, shape, axis) & 3
    q0, q1, q2 = q == 0, q == 1, q == 2
    dl, dh, dy, us, uxs = [], [], [], [], []
    for i in range(3):
        po, plw, prw = own(i), left(i), right(i)
        u, ux = own(3 + i), jnp.where(q1, left(3 + i), right(3 + i))
        bw, aw = shift(po, 1, axis), shift(po, -1, axis)
        bl, ar = shift(plw, 1, axis), shift(prw, -1, axis)
        bc, ac = jnp.where(q2, bl, bw), jnp.where(q1, ar, aw)
        sc, sw = 0.5 * minmod(po - bc, ac - po), 0.5 * minmod(po - bw, aw - po)
        px = jnp.where(q1, plw, prw)
        bx, ax = jnp.where(q1, bl, bw), jnp.where(q1, aw, ar)
        sx = 0.5 * minmod(px - bx, ax - px)
        up, um = c * jnp.maximum(u, 0.0), c * jnp.minimum(u, 0.0)
        dl.append((sc - sw) * up)
        dh.append((sw - sc) * um)
        wrong = jnp.where(q1, (po + sw) * up, (po - sw) * um)
        outer = jnp.where(
            q1, (px + sx) * (c * jnp.maximum(ux, 0.0)), (px - sx) * (c * jnp.minimum(ux, 0.0))
        )
        dy.append((outer, wrong))
        us.append(u)
        uxs.append(ux)
    result = []
    outer, wrong = [d[0] for d in dy], [d[1] for d in dy]
    for k in range(6):
        a, b = total(dl), total(dh)
        y = total(outer) - total(wrong)
        mid = a - b
        result.append(
            jnp.where(
                q0,
                shift(b, -1, axis),
                jnp.where(
                    q1,
                    mid + shift(y, -1, axis),
                    jnp.where(q2, mid - shift(y, 1, axis), -shift(a, 1, axis)),
                ),
            )
        )
        if k < 5:
            dl = [v * u for v, u in zip(dl, us)]
            dh = [v * u for v, u in zip(dh, us)]
            wrong = [v * u for v, u in zip(wrong, us)]
            outer = [v * u for v, u in zip(outer, uxs)]
    return result


def invert(m):
    inv0 = 1.0 / m[0]
    a0 = m[1] * inv0
    s = [None] + [m[l + 1] - a0 * m[l] for l in range(1, 5)]
    inv1 = 1.0 / s[1]
    lead = s[2] * inv1
    a1 = lead - a0
    b1 = s[1] * inv0
    t2 = s[3] - a1 * s[2] - b1 * m[2]
    t3 = s[4] - a1 * s[3] - b1 * m[3]
    inv2 = 1.0 / t2
    a2 = t3 * inv2 - lead
    b2 = t2 * inv1
    centre = (a0 + a1 + a2) * (1.0 / 3.0)
    d0, d1, d2 = a0 - centre, a1 - centre, a2 - centre
    square = (d0 * d0 + d1 * d1 + d2 * d2 + 2.0 * b1 + 2.0 * b2) * (1.0 / 6.0)
    radius = jnp.sqrt(square)
    det = d0 * d1 * d2 - d0 * b2 - d2 * b1
    half = det / (4.0 * square * radius)
    high = centre + 2.0 * radius * third_cos(jnp.sqrt(jnp.maximum(0.5 + half, 0.0)))
    low = centre - 2.0 * radius * third_cos(jnp.sqrt(jnp.maximum(0.5 - half, 0.0)))
    middle = 3.0 * centre - high - low
    ib1, ib2 = m[0] * inv1, s[1] * inv2
    masses = []
    for value in (low, middle, high):
        d = value - a0
        e = (value - a1) * d - b1
        masses.append(m[0] / (1.0 + ib1 * (d * d + ib2 * (e * e))))
    return masses, (low, middle, high)


def kernel(
    sizes, w_hbm, u_hbm, out_hbm, w1, u1, w2, u2, start, mid, acc, outv, ey, ez,
    packy, packz, rx, ry, rz, mx, ra, rb,
    s_in, s_out, sx_s, sx_r, sy_s, sy_r, sz_s, sz_r, sa_s, sa_r, sb_s, sb_r,
):
    ngx, ngy, ngz = sizes
    gx, gy, gz = (lax.axis_index(a) for a in ("gx", "gy", "gz"))
    _, nx, nz, ny = w1.shape
    chunks = nz // ROWS
    xdown, xup = {"gx": lax.rem(gx + ngx - 1, ngx)}, {"gx": lax.rem(gx + 1, ngx)}
    ydown, yup = {"gy": lax.rem(gy + ngy - 1, ngy)}, {"gy": lax.rem(gy + 1, ngy)}
    zdown, zup = {"gz": lax.rem(gz + ngz - 1, ngz)}, {"gz": lax.rem(gz + 1, ngz)}
    peers_a = [{"gx": lax.rem(gx + d, ngx)} for d in range(1, ngx)]
    flat = gy * ngz + gz
    peers_b = []
    for d in range(1, ngy * ngz):
        other = lax.rem(flat + d, ngy * ngz)
        peers_b.append({"gy": lax.div(other, ngz), "gz": lax.rem(other, ngz)})

    loads = [
        pltpu.make_async_copy(w_hbm, w1, s_in.at[0]),
        pltpu.make_async_copy(u_hbm, u1, s_in.at[1]),
    ]
    for copy in loads:
        copy.start()
    barrier = pltpu.get_barrier_semaphore()
    for peer in peers_a + peers_b:
        pl.semaphore_signal(barrier, inc=1, device_id=peer, device_id_type=MESH)
    loads[1].wait()

    def remote(src, dst, send, recv, peer):
        pltpu.make_async_remote_copy(
            src_ref=src, dst_ref=dst, send_sem=send, recv_sem=recv,
            device_id=peer, device_id_type=MESH,
        ).start()

    def wait_bytes(ref, sem):
        pltpu.make_async_copy(ref, ref, sem).wait()

    def send_all(src, peers, dst, send, recv):
        for d, peer in enumerate(peers):
            remote(src, dst.at[d], send, recv, peer)

    def send_x(s, c, w, u):
        rows = pl.ds(pl.multiple_of(c * ROWS, ROWS), ROWS)
        dst, send, recv = rx.at[s, c], sx_s.at[s, c], sx_r.at[s, c]
        remote(w.at[:, 0:2, rows], dst.at[:, 3:5], send, recv, xdown)
        remote(w.at[:, nx - 2 : nx, rows], dst.at[:, 0:2], send, recv, xup)
        remote(u.at[:, 0:1, rows], dst.at[:, 5:6], send, recv, xdown)
        remote(u.at[:, nx - 1 : nx, rows], dst.at[:, 2:3], send, recv, xup)

    def exchange_yz(s, w, u):
        lane = lax.broadcasted_iota(jnp.int32, (ROWS, ny), 1) >> 2

        def pack(c, held):
            rows = pl.ds(pl.multiple_of(c * ROWS, ROWS), ROWS)
            held = list(held)
            for x in range(nx):
                p = c * nx + x
                for i in range(3):
                    for j, ref in ((i, w), (3 + i, u)):
                        moved = pltpu.roll(ref[i, x, rows, :], 4 * p + 2, 1)
                        held[j] = jnp.where(lane == p, moved, held[j])
            return tuple(held)

        held = lax.fori_loop(
            0, chunks, pack, tuple(jnp.zeros((ROWS, ny), jnp.float32) for _ in range(6))
        )
        for j in range(6):
            packy[s, j] = held[j]
        for i in range(3):
            for x in range(nx):
                for j, ref in ((i, w), (3 + i, u)):
                    packz[s, j, 4 * x : 4 * x + 2, :] = ref[i, x, nz - 2 : nz, :]
                    packz[s, j, 4 * x + 2 : 4 * x + 4, :] = ref[i, x, 0:2, :]
        remote(packy.at[s], ry.at[s, 1], sy_s.at[s], sy_r.at[s], ydown)
        remote(packy.at[s], ry.at[s, 0], sy_s.at[s], sy_r.at[s], yup)
        remote(packz.at[s], rz.at[s, 1], sz_s.at[s], sz_r.at[s], zdown)
        remote(packz.at[s], rz.at[s, 0], sz_s.at[s], sz_r.at[s], zup)

    def line_terms(w, u, x, rows, axis, c):
        ls, rs, us = [], [], []
        for i in range(3):
            wv, uv = w[i, x, rows, :], u[i, x, rows, :]
            jump = wv - shift(wv, 1, axis)
            s = 0.5 * minmod(jump, shift(jump, -1, axis))
            ls.append((wv + s) * (c * jnp.maximum(uv, 0.0)))
            rs.append((wv - s) * (c * jnp.minimum(uv, 0.0)))
            us.append(uv)
        for k in range(6):
            g, h = total(ls), total(rs)
            yield k, (g - h) - shift(g, 1, axis) + shift(h, -1, axis)
            if k < 5:
                ls = [v * u_ for v, u_ in zip(ls, us)]
                rs = [v * u_ for v, u_ in zip(rs, us)]

    def interior_z(w, u):
        def body(x, carry):
            for k, d in line_terms(w, u, x, slice(None), 0, CZ):
                acc[k, x] = d
            return carry

        lax.fori_loop(0, nx, body, 0)

    def interior_y(w, u, with_start):
        def body(c, carry):
            rows = pl.ds(pl.multiple_of(c * ROWS, ROWS), ROWS)
            for x in range(nx):
                for k, d in line_terms(w, u, x, rows, 1, CY):
                    acc[k, x, rows, :] += d
                if with_start:
                    power = [w[i, x, rows, :] for i in range(3)]
                    us = [u[i, x, rows, :] for i in range(3)]
                    for k in range(6):
                        start[k, x, rows, :] = total(power)
                        if k < 5:
                            power = [v * u_ for v, u_ in zip(power, us)]
            return carry

        lax.fori_loop(0, chunks, body, 0)

    def edges_yz(s):
        wait_bytes(ry.at[s], sy_r.at[s])
        terms = edge_terms(
            lambda j: packy[s, j], lambda j: ry[s, 0, j], lambda j: ry[s, 1, j], 1, CY
        )
        for k in range(6):
            ey[k] = terms[k]
        wait_bytes(rz.at[s], sz_r.at[s])
        terms = edge_terms(
            lambda j: packz[s, j], lambda j: rz[s, 0, j], lambda j: rz[s, 1, j], 0, CZ
        )
        for k in range(6):
            ez[k] = terms[k]
        for k in range(6):
            for x in range(nx):
                acc[k, x, nz - 2 : nz, :] += ez[k, 4 * x : 4 * x + 2, :]
                acc[k, x, 0:2, :] += ez[k, 4 * x + 2 : 4 * x + 4, :]

    def x_terms(s, c, w, u):
        rows = pl.ds(pl.multiple_of(c * ROWS, ROWS), ROWS)
        lane = lax.broadcasted_iota(jnp.int32, (ROWS, ny), 1)
        edge = (lane < 2) | (lane >= ny - 2)
        ls, rs, us = [], [], []
        for i in range(3):
            wv = [rx[s, c, i, 0], rx[s, c, i, 1]]
            wv += [w[i, x, rows, :] for x in range(nx)]
            wv += [rx[s, c, i, 3], rx[s, c, i, 4]]
            uv = [rx[s, c, i, 2]] + [u[i, x, rows, :] for x in range(nx)] + [rx[s, c, i, 5]]
            jumps = [b - a for a, b in zip(wv[:-1], wv[1:])]
            slopes = [0.5 * minmod(a, b) for a, b in zip(jumps[:-1], jumps[1:])]
            inner = wv[1:-1]
            ls.append([
                (inner[x] + slopes[x]) * (CX * jnp.maximum(uv[x], 0.0)) for x in range(nx + 1)
            ])
            rs.append([
                (inner[x] - slopes[x]) * (CX * jnp.minimum(uv[x], 0.0)) for x in range(1, nx + 2)
            ])
            us.append(uv)
        for k in range(6):
            flux = [
                total([ls[i][x] for i in range(3)]) + total([rs[i][x] for i in range(3)])
                for x in range(nx + 1)
            ]
            for x in range(nx):
                fix = pltpu.roll(ey[k], ny - 2 - 4 * (c * nx + x), 1)
                d = acc[k, x, rows, :] + (flux[x + 1] - flux[x]) + jnp.where(edge, fix, 0.0)
                yield k, x, rows, d
            if k < 5:
                for i in range(3):
                    ls[i] = [v * us[i][x] for x, v in enumerate(ls[i])]
                    rs[i] = [v * us[i][x + 1] for x, v in enumerate(rs[i])]

    def step_of(value):
        return COURANT / (SPEED_TOTAL * jnp.max(value, axis=(0, 1), keepdims=True))

    def tiles_max(value, ref):
        for d in range(ref.shape[0]):
            value = jnp.maximum(value, ref[d])
        return value

    def largest(c, held):
        rows = pl.ds(pl.multiple_of(c * ROWS, ROWS), ROWS)
        for x in range(nx):
            for i in range(3):
                held = jnp.maximum(held, jnp.abs(u1[i, x, rows, :]))
        return held

    zero = jnp.zeros((ROWS, ny), jnp.float32)
    mx[0] = lax.fori_loop(0, chunks, largest, zero)
    loads[0].wait()
    pl.semaphore_wait(barrier, len(peers_a) + len(peers_b))
    send_all(mx.at[0], peers_a, ra.at[0], sa_s.at[0], sa_r.at[0])

    def send_first(c, carry):
        send_x(0, c, w1, u1)
        return carry

    lax.fori_loop(0, chunks, send_first, 0)
    exchange_yz(0, w1, u1)
    interior_z(w1, u1)
    wait_bytes(ra.at[0], sa_r.at[0])
    mx[1] = tiles_max(mx[0], ra.at[0])
    send_all(mx.at[1], peers_b, rb.at[0], sb_s.at[0], sb_r.at[0])
    interior_y(w1, u1, True)
    edges_yz(0)
    wait_bytes(rb.at[0], sb_r.at[0])
    step_one = step_of(tiles_max(mx[1], rb.at[0]))

    def advance(c, held):
        wait_bytes(rx.at[0, c], sx_r.at[0, c])
        rows = pl.ds(pl.multiple_of(c * ROWS, ROWS), ROWS)
        for k, x, rows, d in x_terms(0, c, w1, u1):
            mid[k, x, rows, :] = start[k, x, rows, :] - step_one * d
        for x in range(nx):
            masses, speeds = invert([mid[k, x, rows, :] for k in range(6)])
            for i in range(3):
                w2[i, x, rows, :] = masses[i]
                u2[i, x, rows, :] = speeds[i]
                held = jnp.maximum(held, jnp.abs(speeds[i]))
        send_x(1, c, w2, u2)
        return held

    mx[2] = lax.fori_loop(0, chunks, advance, zero)

    send_all(mx.at[2], peers_b, rb.at[1], sb_s.at[1], sb_r.at[1])
    exchange_yz(1, w2, u2)
    interior_z(w2, u2)
    wait_bytes(rb.at[1], sb_r.at[1])
    mx[3] = tiles_max(mx[2], rb.at[1])
    send_all(mx.at[3], peers_a, ra.at[1], sa_s.at[1], sa_r.at[1])
    interior_y(w2, u2, False)
    edges_yz(1)

    def gather(c, carry):
        wait_bytes(rx.at[1, c], sx_r.at[1, c])
        for k, x, rows, d in x_terms(1, c, w2, u2):
            acc[k, x, rows, :] = d
        return carry

    lax.fori_loop(0, chunks, gather, 0)
    wait_bytes(ra.at[1], sa_r.at[1])
    step_two = step_of(tiles_max(mx[3], ra.at[1]))

    def out_copy(c):
        rows = pl.ds(pl.multiple_of(c * ROWS, ROWS), ROWS)
        return pltpu.make_async_copy(outv.at[:, :, rows], out_hbm.at[:, :, rows], s_out.at[c])

    def finish(c, carry):
        rows = pl.ds(pl.multiple_of(c * ROWS, ROWS), ROWS)
        for k in range(6):
            for x in range(nx):
                at = (k, x, rows, slice(None))
                outv[at] = 0.5 * start[at] + 0.5 * (mid[at] - step_two * acc[at])
        out_copy(c).start()
        return carry

    lax.fori_loop(0, chunks, finish, 0)

    def drain(c, carry):
        out_copy(c).wait()
        for s in range(2):
            wait_bytes(rx.at[s, c], sx_s.at[s, c])
        return carry

    lax.fori_loop(0, chunks, drain, 0)
    for s in range(2):
        wait_bytes(ry.at[s], sy_s.at[s])
        wait_bytes(rz.at[s], sz_s.at[s])
        wait_bytes(ra.at[s], sa_s.at[s])
        wait_bytes(rb.at[s], sb_s.at[s])


def local(sizes, weights, abscissas):
    ngx, ngy, ngz = sizes
    _, nx, nz, ny = weights.shape
    chunks = nz // ROWS
    assert nz % ROWS == 0 and 4 * nx * chunks <= ny and nx >= 2
    assert min(sizes) > 1
    f32 = jnp.float32
    node = pltpu.VMEM((3, nx, nz, ny), f32)
    field = pltpu.VMEM((6, nx, nz, ny), f32)
    dma = pltpu.SemaphoreType.DMA
    na, nb = ngx - 1, ngy * ngz - 1
    any_space = pl.BlockSpec(memory_space=pl.ANY)
    return pl.pallas_call(
        functools.partial(kernel, sizes),
        out_shape=jax.ShapeDtypeStruct((6, nx, nz, ny), f32),
        in_specs=[any_space] * 2,
        out_specs=any_space,
        scratch_shapes=[
            node, node, node, node, field, field, field, field,
            pltpu.VMEM((6, ROWS, ny), f32),
            pltpu.VMEM((6, 4 * nx, ny), f32),
            pltpu.VMEM((2, 6, ROWS, ny), f32),
            pltpu.VMEM((2, 6, 4 * nx, ny), f32),
            pltpu.VMEM((2, chunks, 3, 6, ROWS, ny), f32),
            pltpu.VMEM((2, 2, 6, ROWS, ny), f32),
            pltpu.VMEM((2, 2, 6, 4 * nx, ny), f32),
            pltpu.VMEM((4, ROWS, ny), f32),
            pltpu.VMEM((2, na, ROWS, ny), f32),
            pltpu.VMEM((2, nb, ROWS, ny), f32),
            dma((2,)), dma((chunks,)),
            dma((2, chunks)), dma((2, chunks)),
        ] + [dma((2,))] * 8,
        compiler_params=pltpu.CompilerParams(
            collective_id=0, has_side_effects=True, vmem_limit_bytes=48 * 1024 * 1024
        ),
    )(weights, abscissas)


def solution(mesh):
    sizes = tuple(mesh.shape[a] for a in ("gx", "gy", "gz"))
    spec = P(None, "gx", "gz", "gy")
    return jax.shard_map(
        functools.partial(local, sizes), mesh=mesh, in_specs=(spec, spec), out_specs=spec,
        check_vma=False,
    )
```

time: 211 us -> 39.1 us (0.19)
  blocking collectives: 80.8 us -> 0 us
  other arithmetic: 36.4 us -> 0 us
  Pallas kernels: 0 us -> 36 us
  local copies, waits for them, and re-layouts: 35.6 us -> 2.87 us
  waiting for transfers between devices: 32.5 us -> 0 us
  starting transfers between devices: 22.7 us -> 0 us
  between operations: 2.12 us -> 0.01 us
    pmax x2 -> x0, blocking collectives: 80.8 us -> none  [the longest x1 40.6 us: local(): fastest = lax.pmax(jnp.max(jnp.abs(abscissas)), ('gx', 'gy', 'gz'))]
    pallas_call x0 -> x1, Pallas kernels: none -> 36 us  [local(): pl.pallas_call(functools.partial(kernel, sizes), out_shape=jax.ShapeDtype...]
    ppermute x18 -> x0, waiting for transfers between devices: 32.5 us -> none  [the longest x9 20.6 us: with_halo(): before = lax.ppermute(last, axis, up)]
    ppermute x18 -> x0, starting transfers between devices: 22.7 us -> none  [the longest x9 15.4 us: with_halo(): after = lax.ppermute(initial, axis, down)]
    slice x18 -> x0, local copies, waits for them, and re-layouts: 14.8 us -> none  [the longest x10 9.78 us: with_halo(): last = lax.slice_in_dim(value, length - width, length, axis=dim)]
    unnamed x69 -> x5, local copies, waits for them, and re-layouts: 13 us -> 2.87 us
    div x3 -> x0, other arithmetic: 9.51 us -> none  [invert(): mom[0] / (1.0 + first_comp * first_comp + second_comp * second_comp)]
    ppermute x12 -> x0, local copies, waits for them, and re-layouts: 7 us -> none  [the longest x6 4.09 us: with_halo(): after = lax.ppermute(initial, axis, down)]
  transfers between devices with their start and end apart: 18 -> 0, of which waited for: 10 -> 0; matrix products, arithmetic and copies ran while one was open for 12% -> 0% of each run, Pallas kernels for 0% -> 0%
where the time goes in v1:
time: 39.1 us; the launch traced here: 38.9 us
  Pallas kernels  36 us (92%)
  local copies, waits for them, and re-layouts  2.87 us (7%)
    pallas_call x1, Pallas kernels, local(): pl.pallas_call(functools.partial(kernel, sizes), out_shape=jax.ShapeDtype...  36 us
    unnamed x5, local copies, waits for them, and re-layouts  2.87 us

profile of v1, /device:TPU:0, one launch (start us, length us, event | category | flops | bytes accessed | tf_op | source)
XLA Modules:
  0.0 38.9 jit_solution(10542559718359830285)
XLA Ops:
  0.0 0.0 copy-start
  0.0 1.0 %copy-done = f32[3,4,64,128]{3,2,1,0:T(8,128)S(1)} copy-done((f32[3,4,64,128]{3,2,1,0:T(8,128)S(1)}, f32[3,4,64,128]{3,2,1,0:T(8,128)}, u32[]{:S(2)}) %copy-start) | copy-done | bytes 393240
  1.0 0.0 copy-start.1
  1.0 1.0 %copy-done.1 = f32[3,4,64,128]{3,2,1,0:T(8,128)S(1)} copy-done((f32[3,4,64,128]{3,2,1,0:T(8,128)S(1)}, f32[3,4,64,128]{3,2,1,0:T(8,128)}, u32[]{:S(2)}) %copy-start.1) | copy-done | bytes 393240
  2.0 36.0 %shard_map.28 = f32[6,4,64,128]{3,2,1,0:T(8,128)S(1)} custom-call(f32[3,4,64,128]{3,2,1,0:T(8,128)S(1)} %copy-done, f32[3,4,64,128]{3,2,1,0:T(8,128)S(1)} %copy-done.1), custom_call_target="tpu_custom_call" | custom-call | tf_op jit(solution)/shard_map/pallas_call | solution.py:406
  38.0 0.9 %copy.4 = f32[6,4,64,128]{3,2,1,0:T(8,128)} copy(f32[6,4,64,128]{3,2,1,0:T(8,128)S(1)} %shard_map.28) | data formatting | bytes 1572864
Async XLA Ops:
  0.0 1.0 %copy-start = (f32[3,4,64,128]{3,2,1,0:T(8,128)S(1)}, f32[3,4,64,128]{3,2,1,0:T(8,128)}, u32[]{:S(2)}) copy-start(f32[3,4,64,128]{3,2,1,0:T(8,128)} %w_hbm.1) | copy-start | bytes 1179652
  1.0 1.0 %copy-start.1 = (f32[3,4,64,128]{3,2,1,0:T(8,128)S(1)}, f32[3,4,64,128]{3,2,1,0:T(8,128)}, u32[]{:S(2)}) copy-start(f32[3,4,64,128]{3,2,1,0:T(8,128)} %u_hbm.1) | copy-start | bytes 1179652

commit v2 on v1

--- a/solution.py
+++ b/solution.py
@@ -119,7 +119,7 @@
 
 
 def kernel(
-    sizes, w_hbm, u_hbm, out_hbm, w1, u1, w2, u2, start, mid, acc, outv, ey, ez,
+    sizes, w_hbm, u_hbm, out_hbm, w1, u1, w2, u2, start, mid, acc, out, ey, ez,
     packy, packz, rx, ry, rz, mx, ra, rb,
     s_in, s_out, sx_s, sx_r, sy_s, sy_r, sz_s, sz_r, sa_s, sa_r, sb_s, sb_r,
 ):
@@ -327,6 +327,8 @@
     wait_bytes(rb.at[0], sb_r.at[0])
     step_one = step_of(tiles_max(mx[1], rb.at[0]))
 
+    early = chunks - 2
+
     def advance(c, held):
         wait_bytes(rx.at[0, c], sx_r.at[0, c])
         rows = pl.ds(pl.multiple_of(c * ROWS, ROWS), ROWS)
@@ -338,7 +340,10 @@
                 w2[i, x, rows, :] = masses[i]
                 u2[i, x, rows, :] = speeds[i]
                 held = jnp.maximum(held, jnp.abs(speeds[i]))
-        send_x(1, c, w2, u2)
+        @pl.when(c < early)
+        def _():
+            send_x(1, c, w2, u2)
+
         return held
 
     mx[2] = lax.fori_loop(0, chunks, advance, zero)
@@ -349,29 +354,25 @@
     wait_bytes(rb.at[1], sb_r.at[1])
     mx[3] = tiles_max(mx[2], rb.at[1])
     send_all(mx.at[3], peers_a, ra.at[1], sa_s.at[1], sa_r.at[1])
+    def send_late(c, carry):
+        send_x(1, c, w2, u2)
+        return carry
+
+    lax.fori_loop(early, chunks, send_late, 0)
     interior_y(w2, u2, False)
     edges_yz(1)
-
-    def gather(c, carry):
+    wait_bytes(ra.at[1], sa_r.at[1])
+    step_two = step_of(tiles_max(mx[3], ra.at[1]))
+
+    def out_copy(c):
+        rows = pl.ds(pl.multiple_of(c * ROWS, ROWS), ROWS)
+        return pltpu.make_async_copy(out.at[:, :, rows], out_hbm.at[:, :, rows], s_out.at[c])
+
+    def finish(c, carry):
         wait_bytes(rx.at[1, c], sx_r.at[1, c])
         for k, x, rows, d in x_terms(1, c, w2, u2):
-            acc[k, x, rows, :] = d
-        return carry
-
-    lax.fori_loop(0, chunks, gather, 0)
-    wait_bytes(ra.at[1], sa_r.at[1])
-    step_two = step_of(tiles_max(mx[3], ra.at[1]))
-
-    def out_copy(c):
-        rows = pl.ds(pl.multiple_of(c * ROWS, ROWS), ROWS)
-        return pltpu.make_async_copy(outv.at[:, :, rows], out_hbm.at[:, :, rows], s_out.at[c])
-
-    def finish(c, carry):
-        rows = pl.ds(pl.multiple_of(c * ROWS, ROWS), ROWS)
-        for k in range(6):
-            for x in range(nx):
-                at = (k, x, rows, slice(None))
-                outv[at] = 0.5 * start[at] + 0.5 * (mid[at] - step_two * acc[at])
+            at = (k, x, rows, slice(None))
+            out[at] = 0.5 * start[at] + 0.5 * (mid[at] - step_two * d)
         out_copy(c).start()
         return carry
 
@@ -402,12 +403,11 @@
     field = pltpu.VMEM((6, nx, nz, ny), f32)
     dma = pltpu.SemaphoreType.DMA
     na, nb = ngx - 1, ngy * ngz - 1
-    any_space = pl.BlockSpec(memory_space=pl.ANY)
     return pl.pallas_call(
         functools.partial(kernel, sizes),
         out_shape=jax.ShapeDtypeStruct((6, nx, nz, ny), f32),
-        in_specs=[any_space] * 2,
-        out_specs=any_space,
+        in_specs=[pl.BlockSpec(memory_space=pltpu.HBM)] * 2,
+        out_specs=pl.BlockSpec(memory_space=pltpu.HBM),
         scratch_shapes=[
             node, node, node, node, field, field, field, field,
             pltpu.VMEM((6, ROWS, ny), f32),
@@ -424,7 +424,7 @@
             dma((2, chunks)), dma((2, chunks)),
         ] + [dma((2,))] * 8,
         compiler_params=pltpu.CompilerParams(
-            collective_id=0, has_side_effects=True, vmem_limit_bytes=48 * 1024 * 1024
+            collective_id=0, has_side_effects=True, vmem_limit_bytes=67043328
         ),
     )(weights, abscissas)
 

time: 39.1 us -> 37.9 us (0.969)
  local copies, waits for them, and re-layouts: 2.87 us -> 2.09 us
  Pallas kernels: 36 us -> 35.6 us
    unnamed x5 -> x1, local copies, waits for them, and re-layouts: 2.87 us -> 2.09 us
where the time goes in v2:
time: 37.9 us; the launch traced here: 37.7 us
  Pallas kernels  35.6 us (94%)
  local copies, waits for them, and re-layouts  2.09 us (6%)
    pallas_call x1, Pallas kernels, local(): pl.pallas_call(functools.partial(kernel, sizes), out_shape=jax.ShapeDtype...  35.6 us
    unnamed x1, local copies, waits for them, and re-layouts  2.09 us

profile of v2, /device:TPU:0, one launch (start us, length us, event | category | flops | bytes accessed | tf_op | source)
XLA Modules:
  0.0 37.7 jit_solution(16695030240328276349)
XLA Ops:
  0.0 35.6 %shard_map.28 = f32[6,4,64,128]{3,2,1,0:T(8,128)} custom-call(f32[3,4,64,128]{3,2,1,0:T(8,128)} %w_hbm.1, f32[3,4,64,128]{3,2,1,0:T(8,128)} %u_hbm.1), custom_call_target="tpu_custom_call" | custom-call | tf_op jit(solution)/shard_map/pallas_call | solution.py:406
  35.6 2.1 %copy.4 = f32[6,4,64,128]{3,2,1,0:T(8,128)} copy(f32[6,4,64,128]{3,2,1,0:T(8,128)} %shard_map.28) | data formatting | bytes 1572864

commit v3 on v2

--- a/solution.py
+++ b/solution.py
@@ -119,14 +119,14 @@
 
 
 def kernel(
-    sizes, w_hbm, u_hbm, out_hbm, w1, u1, w2, u2, start, mid, acc, out, ey, ez,
+    sizes, w_hbm, u_hbm, out, n1, n2, start, mid, acc, ey, ez,
     packy, packz, rx, ry, rz, mx, ra, rb,
-    s_in, s_out, sx_s, sx_r, sy_s, sy_r, sz_s, sz_r, sa_s, sa_r, sb_s, sb_r,
+    s_in, sx_s, sx_r, sy_s, sy_r, sz_s, sz_r, sa_s, sa_r, sb_s, sb_r,
 ):
     ngx, ngy, ngz = sizes
     gx, gy, gz = (lax.axis_index(a) for a in ("gx", "gy", "gz"))
-    _, nx, nz, ny = w1.shape
-    chunks = nz // ROWS
+    chunks, planes, _, ny = n1.shape
+    nx, nz = planes // 6, chunks * ROWS
     xdown, xup = {"gx": lax.rem(gx + ngx - 1, ngx)}, {"gx": lax.rem(gx + 1, ngx)}
     ydown, yup = {"gy": lax.rem(gy + ngy - 1, ngy)}, {"gy": lax.rem(gy + 1, ngy)}
     zdown, zup = {"gz": lax.rem(gz + ngz - 1, ngz)}, {"gz": lax.rem(gz + 1, ngz)}
@@ -137,16 +137,23 @@
         other = lax.rem(flat + d, ngy * ngz)
         peers_b.append({"gy": lax.div(other, ngz), "gz": lax.rem(other, ngz)})
 
-    loads = [
-        pltpu.make_async_copy(w_hbm, w1, s_in.at[0]),
-        pltpu.make_async_copy(u_hbm, u1, s_in.at[1]),
-    ]
-    for copy in loads:
-        copy.start()
+    def first(x):
+        late = 3 * (x >= nx // 2) if isinstance(x, int) else jnp.where(x >= nx // 2, 3, 0)
+        return 6 * x + late, 6 * x + 3 - late
+
+    def w_at(x, i):
+        return first(x)[0] + i
+
+    def u_at(x, i):
+        return first(x)[1] + i
+
+    for x in range(nx):
+        for i in range(3):
+            pltpu.make_async_copy(u_hbm.at[i, x], n1.at[:, u_at(x, i)], s_in.at[0]).start()
+            pltpu.make_async_copy(w_hbm.at[i, x], n1.at[:, w_at(x, i)], s_in.at[0]).start()
     barrier = pltpu.get_barrier_semaphore()
     for peer in peers_a + peers_b:
         pl.semaphore_signal(barrier, inc=1, device_id=peer, device_id_type=MESH)
-    loads[1].wait()
 
     def remote(src, dst, send, recv, peer):
         pltpu.make_async_remote_copy(
@@ -161,25 +168,29 @@
         for d, peer in enumerate(peers):
             remote(src, dst.at[d], send, recv, peer)
 
-    def send_x(s, c, w, u):
-        rows = pl.ds(pl.multiple_of(c * ROWS, ROWS), ROWS)
-        dst, send, recv = rx.at[s, c], sx_s.at[s, c], sx_r.at[s, c]
-        remote(w.at[:, 0:2, rows], dst.at[:, 3:5], send, recv, xdown)
-        remote(w.at[:, nx - 2 : nx, rows], dst.at[:, 0:2], send, recv, xup)
-        remote(u.at[:, 0:1, rows], dst.at[:, 5:6], send, recv, xdown)
-        remote(u.at[:, nx - 1 : nx, rows], dst.at[:, 2:3], send, recv, xup)
-
-    def exchange_yz(s, w, u):
+    def send_x(s, c, n):
+        send, recv = sx_s.at[s, c], sx_r.at[s, c]
+        @pl.when(gx == 0)
+        def _():
+            remote(n.at[c, 0:9], rx.at[s, c, 9:18], send, recv, xdown)
+
+        remote(n.at[c, planes - 9 : planes], rx.at[s, c, 0:9], send, recv, xup)
+
+        @pl.when(gx != 0)
+        def _():
+            remote(n.at[c, 0:9], rx.at[s, c, 9:18], send, recv, xdown)
+
+
+    def exchange_yz(s, n):
         lane = lax.broadcasted_iota(jnp.int32, (ROWS, ny), 1) >> 2
 
         def pack(c, held):
-            rows = pl.ds(pl.multiple_of(c * ROWS, ROWS), ROWS)
             held = list(held)
             for x in range(nx):
                 p = c * nx + x
                 for i in range(3):
-                    for j, ref in ((i, w), (3 + i, u)):
-                        moved = pltpu.roll(ref[i, x, rows, :], 4 * p + 2, 1)
+                    for j, at in ((i, w_at(x, i)), (3 + i, u_at(x, i))):
+                        moved = pltpu.roll(n[c, at], 4 * p + 2, 1)
                         held[j] = jnp.where(lane == p, moved, held[j])
             return tuple(held)
 
@@ -190,18 +201,18 @@
             packy[s, j] = held[j]
         for i in range(3):
             for x in range(nx):
-                for j, ref in ((i, w), (3 + i, u)):
-                    packz[s, j, 4 * x : 4 * x + 2, :] = ref[i, x, nz - 2 : nz, :]
-                    packz[s, j, 4 * x + 2 : 4 * x + 4, :] = ref[i, x, 0:2, :]
+                for j, at in ((i, w_at(x, i)), (3 + i, u_at(x, i))):
+                    packz[s, j, 4 * x : 4 * x + 2, :] = n[chunks - 1, at, ROWS - 2 : ROWS, :]
+                    packz[s, j, 4 * x + 2 : 4 * x + 4, :] = n[0, at, 0:2, :]
         remote(packy.at[s], ry.at[s, 1], sy_s.at[s], sy_r.at[s], ydown)
         remote(packy.at[s], ry.at[s, 0], sy_s.at[s], sy_r.at[s], yup)
         remote(packz.at[s], rz.at[s, 1], sz_s.at[s], sz_r.at[s], zdown)
         remote(packz.at[s], rz.at[s, 0], sz_s.at[s], sz_r.at[s], zup)
 
-    def line_terms(w, u, x, rows, axis, c):
+    def line_terms(load, axis, c):
         ls, rs, us = [], [], []
         for i in range(3):
-            wv, uv = w[i, x, rows, :], u[i, x, rows, :]
+            wv, uv = load(i)
             jump = wv - shift(wv, 1, axis)
             s = 0.5 * minmod(jump, shift(jump, -1, axis))
             ls.append((wv + s) * (c * jnp.maximum(uv, 0.0)))
@@ -214,23 +225,30 @@
                 ls = [v * u_ for v, u_ in zip(ls, us)]
                 rs = [v * u_ for v, u_ in zip(rs, us)]
 
-    def interior_z(w, u):
+    def interior_z(n):
         def body(x, carry):
-            for k, d in line_terms(w, u, x, slice(None), 0, CZ):
+            def load(i):
+                column = (nz, ny)
+                return n[:, w_at(x, i)].reshape(column), n[:, u_at(x, i)].reshape(column)
+
+            for k, d in line_terms(load, 0, CZ):
                 acc[k, x] = d
             return carry
 
         lax.fori_loop(0, nx, body, 0)
 
-    def interior_y(w, u, with_start):
+    def interior_y(n, with_start):
         def body(c, carry):
             rows = pl.ds(pl.multiple_of(c * ROWS, ROWS), ROWS)
             for x in range(nx):
-                for k, d in line_terms(w, u, x, rows, 1, CY):
+                def load(i, x=x):
+                    return n[c, w_at(x, i)], n[c, u_at(x, i)]
+
+                for k, d in line_terms(load, 1, CY):
                     acc[k, x, rows, :] += d
                 if with_start:
-                    power = [w[i, x, rows, :] for i in range(3)]
-                    us = [u[i, x, rows, :] for i in range(3)]
+                    power = [n[c, w_at(x, i)] for i in range(3)]
+                    us = [n[c, u_at(x, i)] for i in range(3)]
                     for k in range(6):
                         start[k, x, rows, :] = total(power)
                         if k < 5:
@@ -257,16 +275,16 @@
                 acc[k, x, nz - 2 : nz, :] += ez[k, 4 * x : 4 * x + 2, :]
                 acc[k, x, 0:2, :] += ez[k, 4 * x + 2 : 4 * x + 4, :]
 
-    def x_terms(s, c, w, u):
+    def x_terms(s, c, n):
         rows = pl.ds(pl.multiple_of(c * ROWS, ROWS), ROWS)
         lane = lax.broadcasted_iota(jnp.int32, (ROWS, ny), 1)
         edge = (lane < 2) | (lane >= ny - 2)
         ls, rs, us = [], [], []
         for i in range(3):
-            wv = [rx[s, c, i, 0], rx[s, c, i, 1]]
-            wv += [w[i, x, rows, :] for x in range(nx)]
-            wv += [rx[s, c, i, 3], rx[s, c, i, 4]]
-            uv = [rx[s, c, i, 2]] + [u[i, x, rows, :] for x in range(nx)] + [rx[s, c, i, 5]]
+            wv = [rx[s, c, i], rx[s, c, 6 + i]]
+            wv += [n[c, w_at(x, i)] for x in range(nx)]
+            wv += [rx[s, c, 9 + i], rx[s, c, 15 + i]]
+            uv = [rx[s, c, 3 + i]] + [n[c, u_at(x, i)] for x in range(nx)] + [rx[s, c, 12 + i]]
             jumps = [b - a for a, b in zip(wv[:-1], wv[1:])]
             slopes = [0.5 * minmod(a, b) for a, b in zip(jumps[:-1], jumps[1:])]
             inner = wv[1:-1]
@@ -300,29 +318,28 @@
         return value
 
     def largest(c, held):
-        rows = pl.ds(pl.multiple_of(c * ROWS, ROWS), ROWS)
         for x in range(nx):
             for i in range(3):
-                held = jnp.maximum(held, jnp.abs(u1[i, x, rows, :]))
+                held = jnp.maximum(held, jnp.abs(n1[c, u_at(x, i)]))
         return held
 
     zero = jnp.zeros((ROWS, ny), jnp.float32)
+    wait_bytes(n1, s_in.at[0])
     mx[0] = lax.fori_loop(0, chunks, largest, zero)
-    loads[0].wait()
     pl.semaphore_wait(barrier, len(peers_a) + len(peers_b))
     send_all(mx.at[0], peers_a, ra.at[0], sa_s.at[0], sa_r.at[0])
 
     def send_first(c, carry):
-        send_x(0, c, w1, u1)
+        send_x(0, c, n1)
         return carry
 
     lax.fori_loop(0, chunks, send_first, 0)
-    exchange_yz(0, w1, u1)
-    interior_z(w1, u1)
+    exchange_yz(0, n1)
+    interior_z(n1)
     wait_bytes(ra.at[0], sa_r.at[0])
     mx[1] = tiles_max(mx[0], ra.at[0])
     send_all(mx.at[1], peers_b, rb.at[0], sb_s.at[0], sb_r.at[0])
-    interior_y(w1, u1, True)
+    interior_y(n1, True)
     edges_yz(0)
     wait_bytes(rb.at[0], sb_r.at[0])
     step_one = step_of(tiles_max(mx[1], rb.at[0]))
@@ -332,54 +349,48 @@
     def advance(c, held):
         wait_bytes(rx.at[0, c], sx_r.at[0, c])
         rows = pl.ds(pl.multiple_of(c * ROWS, ROWS), ROWS)
-        for k, x, rows, d in x_terms(0, c, w1, u1):
+        for k, x, rows, d in x_terms(0, c, n1):
             mid[k, x, rows, :] = start[k, x, rows, :] - step_one * d
         for x in range(nx):
             masses, speeds = invert([mid[k, x, rows, :] for k in range(6)])
             for i in range(3):
-                w2[i, x, rows, :] = masses[i]
-                u2[i, x, rows, :] = speeds[i]
+                n2[c, w_at(x, i)] = masses[i]
+                n2[c, u_at(x, i)] = speeds[i]
                 held = jnp.maximum(held, jnp.abs(speeds[i]))
         @pl.when(c < early)
         def _():
-            send_x(1, c, w2, u2)
+            send_x(1, c, n2)
 
         return held
 
     mx[2] = lax.fori_loop(0, chunks, advance, zero)
 
     send_all(mx.at[2], peers_b, rb.at[1], sb_s.at[1], sb_r.at[1])
-    exchange_yz(1, w2, u2)
-    interior_z(w2, u2)
+    exchange_yz(1, n2)
+    interior_z(n2)
     wait_bytes(rb.at[1], sb_r.at[1])
     mx[3] = tiles_max(mx[2], rb.at[1])
     send_all(mx.at[3], peers_a, ra.at[1], sa_s.at[1], sa_r.at[1])
     def send_late(c, carry):
-        send_x(1, c, w2, u2)
+        send_x(1, c, n2)
         return carry
 
     lax.fori_loop(early, chunks, send_late, 0)
-    interior_y(w2, u2, False)
+    interior_y(n2, False)
     edges_yz(1)
     wait_bytes(ra.at[1], sa_r.at[1])
     step_two = step_of(tiles_max(mx[3], ra.at[1]))
 
-    def out_copy(c):
-        rows = pl.ds(pl.multiple_of(c * ROWS, ROWS), ROWS)
-        return pltpu.make_async_copy(out.at[:, :, rows], out_hbm.at[:, :, rows], s_out.at[c])
-
     def finish(c, carry):
         wait_bytes(rx.at[1, c], sx_r.at[1, c])
-        for k, x, rows, d in x_terms(1, c, w2, u2):
+        for k, x, rows, d in x_terms(1, c, n2):
             at = (k, x, rows, slice(None))
             out[at] = 0.5 * start[at] + 0.5 * (mid[at] - step_two * d)
-        out_copy(c).start()
         return carry
 
     lax.fori_loop(0, chunks, finish, 0)
 
     def drain(c, carry):
-        out_copy(c).wait()
         for s in range(2):
             wait_bytes(rx.at[s, c], sx_s.at[s, c])
         return carry
@@ -396,37 +407,37 @@
     ngx, ngy, ngz = sizes
     _, nx, nz, ny = weights.shape
     chunks = nz // ROWS
-    assert nz % ROWS == 0 and 4 * nx * chunks <= ny and nx >= 2
+    assert nz % ROWS == 0 and 4 * nx * chunks <= ny and nx >= 4
     assert min(sizes) > 1
     f32 = jnp.float32
-    node = pltpu.VMEM((3, nx, nz, ny), f32)
+    node = pltpu.VMEM((chunks, 6 * nx, ROWS, ny), f32)
     field = pltpu.VMEM((6, nx, nz, ny), f32)
     dma = pltpu.SemaphoreType.DMA
     na, nb = ngx - 1, ngy * ngz - 1
     return pl.pallas_call(
         functools.partial(kernel, sizes),
-        out_shape=jax.ShapeDtypeStruct((6, nx, nz, ny), f32),
+        out_shape=pltpu.VMEM((6, nx, nz, ny), f32),
         in_specs=[pl.BlockSpec(memory_space=pltpu.HBM)] * 2,
-        out_specs=pl.BlockSpec(memory_space=pltpu.HBM),
+        out_specs=pl.BlockSpec(memory_space=pltpu.VMEM),
         scratch_shapes=[
-            node, node, node, node, field, field, field, field,
+            node, node, field, field, field,
             pltpu.VMEM((6, ROWS, ny), f32),
             pltpu.VMEM((6, 4 * nx, ny), f32),
             pltpu.VMEM((2, 6, ROWS, ny), f32),
             pltpu.VMEM((2, 6, 4 * nx, ny), f32),
-            pltpu.VMEM((2, chunks, 3, 6, ROWS, ny), f32),
+            pltpu.VMEM((2, chunks, 18, ROWS, ny), f32),
             pltpu.VMEM((2, 2, 6, ROWS, ny), f32),
             pltpu.VMEM((2, 2, 6, 4 * nx, ny), f32),
             pltpu.VMEM((4, ROWS, ny), f32),
             pltpu.VMEM((2, na, ROWS, ny), f32),
             pltpu.VMEM((2, nb, ROWS, ny), f32),
-            dma((2,)), dma((chunks,)),
+            dma((2,)),
             dma((2, chunks)), dma((2, chunks)),
         ] + [dma((2,))] * 8,
         compiler_params=pltpu.CompilerParams(
-            collective_id=0, has_side_effects=True, vmem_limit_bytes=67043328
+            collective_id=0, has_side_effects=True, vmem_limit_bytes=56000000
         ),
-    )(weights, abscissas)
+    )(*(a.reshape(3, nx, chunks, ROWS, ny) for a in (weights, abscissas)))
 
 
 def solution(mesh):

time: 37.9 us -> 35.7 us (0.942)
  local copies, waits for them, and re-layouts: 2.09 us -> 0.88 us
  Pallas kernels: 35.6 us -> 34.6 us
    unnamed x1, local copies, waits for them, and re-layouts: 2.09 us -> 0.88 us
    pallas_call x1, Pallas kernels: 35.6 us -> 34.6 us  [local(): pl.pallas_call(functools.partial(kernel, sizes), out_shape=pltpu.VMEM((6,...]
where the time goes in v3:
time: 35.7 us; the launch traced here: 35.5 us
  Pallas kernels  34.6 us (97%)
  local copies, waits for them, and re-layouts  0.88 us (2%)
    pallas_call x1, Pallas kernels, local(): pl.pallas_call(functools.partial(kernel, sizes), out_shape=pltpu.VMEM((6,...  34.6 us
    unnamed x1, local copies, waits for them, and re-layouts  0.88 us

profile of v3, /device:TPU:0, one launch (start us, length us, event | category | flops | bytes accessed | tf_op | source)
XLA Modules:
  0.0 35.5 jit_solution(11057154994211048419)
XLA Ops:
  0.0 34.6 %shard_map.28 = f32[6,4,64,128]{3,2,1,0:T(8,128)S(1)} custom-call(f32[3,4,8,8,128]{4,3,2,1,0:T(8,128)} %bitcast.2, f32[3,4,8,8,128]{4,3,2,1,0:T(8,128)} %bitcast.3), custom_call_target="tpu_custom_call" | custom-call | tf_op jit(solution)/shard_map/pallas_call | solution.py:417
  34.6 0.9 %copy.4 = f32[6,4,64,128]{3,2,1,0:T(8,128)} copy(f32[6,4,64,128]{3,2,1,0:T(8,128)S(1)} %shard_map.28) | data formatting | bytes 1572864
